TPU v7x, 32 devices: a whole 2x2x4 slice. The times are simulated.
32 devices in a mesh: cp: 4 (over z), dp: 8 (over y, x, core).
Axes of the slice: x: 2, y: 2, z: 4, core: 2. Of those that a mesh axis runs over, the one named last changes fastest.
Arguments:
- tokens: bfloat16 [32, 1536, 7168], P('dp', 'cp')
- choices: int32 [32, 1536, 8], P('dp', 'cp')
- router_w: float32 [384, 7168], replicated
- expert_bias: float32 [384], replicated
Outputs:
- output 1: float32 [], replicated
- output 2: float32 [384, 7168], replicated
- output 3: bfloat16 [32, 1536, 7168], P('dp', 'cp')
- output 4: float32 [384], replicated
All inputs are finite; a program needn't handle non-finite values.
Results may differ from a plain program's by a relative error of at most 0.001.
Values sent between devices are 32-bit elements.
A program may use at most 1 GiB of HBM per device.

v0:
```python
import jax
import jax.numpy as jnp
from jax import lax
from jax.sharding import PartitionSpec as P

ALPHA = 0.1
GAMMA = 0.001
PRECISE = lax.Precision.HIGHEST


def solution(mesh):
    cp_size = mesh.shape["cp"]
    dp_size = mesh.shape["dp"]

    def local_step(tokens, choices, router_w, expert_bias):
        rows_all = tokens.shape[0] * dp_size
        seq_all = tokens.shape[1] * cp_size
        experts = router_w.shape[0]
        choice_num = choices.shape[2]
        expert_ids = jnp.arange(experts, dtype=jnp.int32)
        piece_counts = jnp.sum((choices[..., None] == expert_ids).astype(jnp.float32), axis=(1, 2))
        seq_counts = lax.psum(piece_counts, "cp")
        logits = jnp.einsum("bsd,nd->bsn", tokens, router_w, precision=PRECISE, preferred_element_type=jnp.float32)
        sig_probs = jax.nn.sigmoid(logits)
        prob_total = jnp.sum(sig_probs, axis=-1, keepdims=True)
        normed = sig_probs / prob_total
        prob_sums = lax.psum(jnp.sum(normed, axis=1), "cp")
        loss_scale = ALPHA * experts / (rows_all * choice_num * seq_all * seq_all)
        weight = seq_counts * loss_scale
        bal_loss = lax.psum(jnp.sum(weight * prob_sums), "dp")
        mixed_grad = jnp.sum(normed * weight[:, None, :], axis=-1, keepdims=True)
        grad_logits = (weight[:, None, :] - mixed_grad) * (sig_probs * (1.0 - sig_probs) / prob_total)
        grad_tokens = jnp.einsum("bsn,nd->bsd", grad_logits, router_w, precision=PRECISE, preferred_element_type=jnp.float32).astype(jnp.bfloat16)
        grad_part = jnp.einsum("bsn,bsd->nd", grad_logits, tokens, precision=PRECISE, preferred_element_type=jnp.float32)
        grad_router = lax.psum(grad_part, ("cp", "dp"))
        global_load = lax.psum(jnp.sum(seq_counts, axis=0), "dp")
        load_gap = rows_all * seq_all * choice_num - experts * global_load.astype(jnp.int32)
        new_bias = expert_bias + GAMMA * jnp.sign(load_gap).astype(jnp.float32)
        return bal_loss, grad_router, grad_tokens, new_bias

    tok_spec = P("dp", "cp", None)
    return jax.shard_map(local_step, mesh=mesh, in_specs=(tok_spec, tok_spec, P(), P()), out_specs=(P(), P(), tok_spec, P()), check_vma=False)
```

profile of v0, /device:TPU:0, one launch (start us, length us, event | category | flops | bytes accessed | tf_op | source)
XLA Modules:
  0.0 320.5 jit_solution(8739427037681576120)
XLA Ops:
  7.2 0.0 all-reduce.3.cloned.1.call-start
  7.2 1.1 copy.10
  8.3 2.5 convert_reduce_fusion
  10.8 13.7 %psum.35 = f32[4,384]{1,0:T(4,128)S(1)} all-reduce(f32[4,384]{1,0:T(4,128)S(1)} %convert_reduce_fusion), channel_id=1, replica_groups=mesh['cp'=4,'dp'=8] {'cp'}, use_global_device_ids=true, to_apply=%region_1.0 | all-reduce | flops 1536 | bytes 12288 | tf_op jit(solution)/shard_map/psum | solution.py:22
  24.5 30.8 %fusion.6 = (f32[4,384]{1,0:T(4,128)S(1)}, f32[4,384,384]{1,2,0:T(8,128)S(1)}) fusion(bf16[4,384,7168]{2,1,0:T(8,128)(2,1)} %param.4, f32[384,7168]{1,0:T(8,128)} %param.6), kind=kOutput, calls=%fused_computation.14 | convolution fusion | flops 50736660480 | bytes 35395584 | tf_op jit(solution)/shard_map/bsd,nd->bsn/dot_general | solution.py:23
  55.3 0.9 multiply_reduce_fusion
  56.2 34.0 %convolution_bitcast_fusion = f32[384,7168]{1,0:T(8,128)} fusion(bf16[4,384,7168]{2,1,0:T(8,128)(2,1)} %param.4, f32[4,384]{1,0:T(4,128)S(1)} %get-tuple-element.4, f32[4,384]{1,0:T(4,128)S(1)} %broadcast_multiply_fusion, f32[4,384]{1,0:T(4,128)S(1)} %get-tuple-element.10, f32[4,384,384]{1,2,0:T(8,128)S(1)} %get-tuple-element.11), kind=kOutput, calls=%fused_computation.6 | convolution fusion | flops 50739019776 | bytes 35407872 | tf_op jit(solution)/shard_map/bsn,bsd->nd/dot_general | solution.py:34
  90.2 0.0 copy-start
  90.2 0.0 all-reduce.3.cloned.1.call-update
  90.2 8.7 %psum.36 = f32[4,384]{1,0:T(4,128)S(1)} all-reduce(f32[4,384]{1,0:T(4,128)S(1)} %get-tuple-element.5), channel_id=1, replica_groups=mesh['cp'=4,'dp'=8] {'cp'}, use_global_device_ids=true, to_apply=%region_4.0 | all-reduce | flops 1536 | bytes 12288 | tf_op jit(solution)/shard_map/psum | solution.py:27
  98.9 0.6 fusion.10
  99.5 12.8 %all-reduce = (f32[]{:T(128)}, f32[384]{0:T(512)S(1)}) all-reduce(f32[]{:T(128)} %get-tuple-element.7, f32[384]{0:T(512)S(1)} %get-tuple-element.6), channel_id=1, replica_groups=mesh['cp'=4,'dp'=8] {'dp'}, use_global_device_ids=true, to_apply=%region_6.0 | all-reduce | flops 385 | bytes 3080 | tf_op jit(solution)/shard_map/psum | solution.py:30
  112.3 0.0 copy-done
  112.3 0.6 multiply_add_fusion
  112.9 77.1 %convolution_convert_fusion = bf16[4,384,7168]{2,1,0:T(8,128)(2,1)} fusion(f32[384,7168]{1,0:T(8,128)} %param.6, f32[4,384]{1,0:T(4,128)S(1)} %get-tuple-element.4, f32[4,384]{1,0:T(4,128)S(1)} %broadcast_multiply_fusion, f32[4,384]{1,0:T(4,128)S(1)} %get-tuple-element.10, f32[4,384,384]{1,2,0:T(8,128)S(1)} %get-tuple-element.11), kind=kOutput, calls=%fused_computation.2 | convolution fusion | flops 50750029824 | bytes 35407872 | tf_op jit(solution)/shard_map/bsn,nd->bsd/dot_general | solution.py:33
  190.0 114.0 %all-reduce.3.cloned.1.call-done = f32[384,7168]{1,0:T(8,128)} async-done(((f32[384,7168]{1,0:T(8,128)}), f32[384,7168]{1,0:T(8,128)}) %all-reduce.3.cloned.1.call-update) | async-done | bytes 11010064 | tf_op jit(solution)/shard_map/psum | solution.py:35
  304.0 9.6 %copy.14 = f32[384,7168]{1,0:T(8,128)} copy(f32[384,7168]{1,0:T(8,128)} %all-reduce.3.cloned.1.call-done) | data formatting | bytes 22020096
  (1 shorter events, 0.0 us)
Async XLA Ops:
  7.2 296.9 %all-reduce.3.cloned.1.call-start = ((), (), s32[]{:S(2)}) async-start(), calls=%async_computation | async-start | bytes 22020096 | tf_op jit(solution)/shard_map/psum | solution.py:35
  90.2 22.1 %copy-start = (f32[384]{0:T(512)S(1)}, f32[384]{0:T(512)}, u32[]{:S(2)}) copy-start(f32[384]{0:T(512)} %param.7) | copy-start | bytes 4612
Sparse Core Ops, SparseCore 0:
  90.4 213.6 all-reduce.2
where the time goes:
time: 321 us
  matrix products  142 us (44%)
  waiting for transfers between devices  114 us (36%)
  blocking collectives  35.2 us (11%)
  between operations  14.1 us (4%)
  local copies, waits for them, and re-layouts  10.7 us (3%)
  other arithmetic  4.59 us (1%)
    psum x1, waiting for transfers between devices, local_step(): grad_router = lax.psum(grad_part, ('cp', 'dp'))  114 us
    dot_general x1, matrix products, local_step(): jnp.einsum('bsn,nd->bsd', grad_logits, router_w, precision=PRECISE, prefe...  77.1 us
    dot_general x1, matrix products, local_step(): jnp.einsum('bsn,bsd->nd', grad_logits, tokens, precision=PRECISE, preferr...  34 us
    dot_general x1, matrix products, local_step(): jnp.einsum('bsd,nd->bsn', tokens, router_w, precision=PRECISE, preferred_...  30.8 us
    psum x1, blocking collectives, local_step(): seq_counts = lax.psum(piece_counts, 'cp')  13.7 us
    psum x1, blocking collectives, local_step(): bal_loss = lax.psum(jnp.sum(weight * prob_sums), 'dp')  12.8 us
    unnamed x4, local copies, waits for them, and re-layouts  10.7 us
    psum x1, blocking collectives, local_step(): prob_sums = lax.psum(jnp.sum(normed, axis=1), 'cp')  8.68 us
  transfers between devices with their start and end apart: 1, of which 1 were waited for; matrix products, arithmetic and copies ran while one was open for 24% of the time, Pallas kernels for 0%

commit v1 on v0

v1 whole, which is shorter than its diff:
```python
import functools

import jax
import jax.numpy as jnp
from jax import lax
from jax.experimental import pallas as pl
from jax.experimental.pallas import tpu as pltpu
from jax.sharding import PartitionSpec as P

ALPHA = 0.1
GAMMA = 0.001
MESH = pl.DeviceIdType.MESH
ANY = pl.BlockSpec(memory_space=pl.ANY)
VMEM = pl.BlockSpec(memory_space=pltpu.VMEM)
COLS = 512
LEVELS = 5
WAIT_RS = (2, 4, 6, 8, 10)
WAIT_AG = (20, 18, 16, 14, 12)


def pieces(val):
    hi = val.astype(jnp.bfloat16)
    rest = val - hi.astype(jnp.float32)
    mid = rest.astype(jnp.bfloat16)
    low = (rest - mid.astype(jnp.float32)).astype(jnp.bfloat16)
    return hi, mid, low


def weight_stack(w, stack, order=(0, 1, 0, 2, 1, 0)):
    experts = w.shape[0]
    parts = pieces(w)
    for k, which in enumerate(order):
        stack[pl.ds(k * experts, experts), :] = parts[which]


def main_kernel(n_dx, seqs, scale, cnt_ref, x_ref, w_ref, dw_ref, dx_ref, cols_out, small_out,
                acc, full, got0, got1, got2, got3, got4, xbuf, wbuf, stack, scores, rows_ref, cols_ref,
                cnt_cur, cnt_got, small_cur, small_got,
                rs_send, rs_recv, ag_send, ag_recv, sm_send, sm_recv, cnt_send, cnt_recv,
                x_sem, w_sem, o_sem, d_sem, c_sem):
    n_chunk, experts = acc.shape[0], acc.shape[1]
    tok_n = xbuf.shape[1]
    seq = tok_n // seqs
    z, dp = lax.axis_index("cp"), lax.axis_index("dp")
    core, xb, yb = dp % 2, (dp // 2) % 2, dp // 4
    zl, zh = z % 2, z // 2
    by_core = (z, dp + 1 - 2 * core)
    by_x = (z, dp + 2 - 4 * xb)
    by_y = (z, dp + 4 - 8 * yb)
    by_zl = (z + 1 - 2 * zl, dp)
    by_zh = (z + 2 - 4 * zh, dp)
    first = (z, dp + (1 - core) * (2 - 4 * xb) + core * (4 - 8 * yb))
    second = (z, dp + core * (2 - 4 * xb) + (1 - core) * (4 - 8 * yb))
    peers = (by_core, first, by_zl, second, by_zh)
    bits = (core, (1 - core) * xb + core * yb, zl, (1 - core) * yb + core * xb, zh)
    got = (got0, got1, got2, got3, got4)

    barrier = pltpu.get_barrier_semaphore()
    for peer in (by_core, by_x, by_y, by_zl, by_zh):
        pl.semaphore_signal(barrier, inc=1, device_id=peer, device_id_type=MESH)

    size, keep, away, base = experts, [], [], 0
    for level in range(LEVELS - 1):
        size //= 2
        keep.append((pl.multiple_of(base + bits[level] * size, 8), size, 0, COLS))
        away.append((pl.multiple_of(base + (1 - bits[level]) * size, 8), size, 0, COLS))
        base = base + bits[level] * size
    half = COLS // 2
    row = pl.multiple_of(base, 8)
    keep.append((row, size, pl.multiple_of(zh * half, 128), half))
    away.append((row, size, pl.multiple_of((1 - zh) * half, 128), half))

    def region(ref, c, where):
        r, n, k, m = where
        return ref.at[c, pl.ds(r, n), pl.ds(k, m)]

    def rs_copy(level, c):
        return pltpu.make_async_remote_copy(
            src_ref=region(acc, c, away[level]), dst_ref=got[level].at[c], send_sem=rs_send.at[level, c],
            recv_sem=rs_recv.at[level, c], device_id=peers[level], device_id_type=MESH)

    def ag_copy(level, c):
        return pltpu.make_async_remote_copy(
            src_ref=region(full, c, keep[level]), dst_ref=region(full, c, keep[level]), send_sem=ag_send.at[level, c],
            recv_sem=ag_recv.at[level, c], device_id=peers[level], device_id_type=MESH)

    def sm_copy(level):
        return pltpu.make_async_remote_copy(
            src_ref=small_cur.at[level], dst_ref=small_got.at[level], send_sem=sm_send.at[level],
            recv_sem=sm_recv.at[level], device_id=(by_core, by_x, by_zl, by_y, by_zh)[level],
            device_id_type=MESH)

    def cnt_copy(k):
        return pltpu.make_async_remote_copy(
            src_ref=cnt_cur.at[k], dst_ref=cnt_got.at[k], send_sem=cnt_send.at[k],
            recv_sem=cnt_recv.at[k], device_id=(by_zl, by_zh)[k], device_id_type=MESH)

    def x_load(c):
        return pltpu.make_async_copy(
            x_ref.at[:, pl.ds(pl.multiple_of(c * COLS, COLS), COLS)], xbuf.at[c % 2], x_sem.at[c % 2])

    def w_load(j):
        return pltpu.make_async_copy(
            w_ref.at[:, pl.ds(pl.multiple_of(j * COLS, COLS), COLS)], wbuf.at[j % 2], w_sem.at[j % 2])

    def dx_store(j):
        return pltpu.make_async_copy(xbuf.at[j % 2], dx_ref.at[j], o_sem.at[j % 2])

    def dw_store(c):
        return pltpu.make_async_copy(full.at[c], dw_ref.at[c], d_sem.at[c])

    x_load(0).start()
    x_load(1).start()
    w_load(0).start()
    w_load(1).start()
    cnt_cur[0] = cnt_ref[...]
    scores[...] = jnp.zeros_like(scores)
    pl.semaphore_wait(barrier, LEVELS)
    cnt_copy(0).start()

    def score_step(i, carry):
        w_load(i).wait()
        weight_stack(wbuf[i % 2], stack, (0, 1, 2))
        x_load(i).wait()
        for t in range(0, tok_n, COLS):
            out = lax.dot_general(
                stack[pl.ds(0, 3 * experts), :], xbuf[i % 2, pl.ds(t, COLS), :], (((1,), (1,)), ((), ())),
                preferred_element_type=jnp.float32)
            scores[:, pl.ds(t, COLS)] += out[:experts] + (out[experts:2 * experts] + out[2 * experts:])
        after = (i + 2) % n_chunk
        x_load(after).start()
        w_load(after).start()

        @pl.when(i == n_chunk // 2)
        def _():
            cnt_copy(0).wait_send()
            cnt_copy(0).wait_recv()
            cnt_cur[1] = cnt_cur[0] + cnt_got[0]
            cnt_copy(1).start()

        return carry

    lax.fori_loop(0, n_chunk, score_step, 0)
    cnt_copy(1).wait_send()
    cnt_copy(1).wait_recv()
    cnt_cur[2] = cnt_cur[1] + cnt_got[1]
    small_cur[0] = jnp.zeros_like(small_cur[0])

    def grad_step(r, carry):
        span = pl.ds(pl.multiple_of(r * seq, seq), seq)
        place = lax.broadcasted_iota(jnp.int32, (experts, experts), 0)
        diag = place == lax.broadcasted_iota(jnp.int32, (experts, experts), 1)
        weight = jnp.sum(jnp.where(diag, cnt_cur[2, pl.ds(r, 1), :], 0.0), axis=1, keepdims=True) * scale
        sig = jax.nn.sigmoid(scores[:, span])
        total = jnp.sum(sig, axis=0, keepdims=True)
        normed = sig / total
        mixed = jnp.sum(normed * weight, axis=0, keepdims=True)
        grad = (weight - mixed) * (sig * (1.0 - sig) / total)
        for k, part in enumerate(pieces(grad)):
            rows_ref[pl.ds(k * experts, experts), span] = part
        turned = pieces(grad.T)
        for k, which in enumerate((0, 0, 1, 0, 1, 2)):
            cols_ref[span, pl.ds(k * experts, experts)] = turned[which]
        loss = jnp.sum(mixed, axis=1, keepdims=True)
        row_id = lax.broadcasted_iota(jnp.int32, (8, experts), 0)
        loads = cnt_ref[pl.ds(r, 1), :]
        small_cur[0] += jnp.where(row_id == 0, loads, jnp.where(row_id == 1, loss, 0.0))
        return carry

    lax.fori_loop(0, seqs, grad_step, 0)
    cols_copy = pltpu.make_async_copy(cols_ref, cols_out, c_sem)
    cols_copy.start()

    def step(i, carry):
        def at(offset):
            c = i - offset
            return c, jnp.logical_and(c >= 0, c < n_chunk)

        for level in range(LEVELS):
            c, live = at(WAIT_AG[level])

            @pl.when(live)
            def _(level=level, c=c):
                copy = ag_copy(level, c)
                copy.wait_send()
                copy.wait_recv()
                if level > 0:
                    ag_copy(level - 1, c).start()
                else:
                    dw_store(c).start()

        for level in reversed(range(LEVELS)):
            c, live = at(WAIT_RS[level])

            @pl.when(live)
            def _(level=level, c=c):
                copy = rs_copy(level, c)
                copy.wait_send()
                copy.wait_recv()
                r, n, k, m = keep[level]
                total = acc[c, pl.ds(r, n), pl.ds(k, m)] + got[level][c]
                if level < LEVELS - 1:
                    acc[c, pl.ds(r, n), pl.ds(k, m)] = total
                    rs_copy(level + 1, c).start()
                else:
                    full[c, pl.ds(r, n), pl.ds(k, m)] = total
                    ag_copy(level, c).start()

        for level in range(LEVELS + 1):
            @pl.when(i == 2 * level)
            def _(level=level):
                if level > 0:
                    copy = sm_copy(level - 1)
                    copy.wait_send()
                    copy.wait_recv()
                    total = small_cur[level - 1] + small_got[level - 1]
                    if level < LEVELS:
                        small_cur[level] = total
                    else:
                        small_out[...] = total
                if level < LEVELS:
                    sm_copy(level).start()

        @pl.when(i < n_chunk)
        def _():
            x_load(i).wait()
            out = jnp.dot(rows_ref[...], xbuf[i % 2], preferred_element_type=jnp.float32)
            acc[i] = out[:experts] + (out[experts:2 * experts] + out[2 * experts:])
            rs_copy(0, i).start()

            @pl.when(i + 2 < n_chunk)
            def _():
                x_load(i + 2).start()

        @pl.when(jnp.logical_and(i >= n_chunk, i < n_chunk + n_dx))
        def _():
            j = i - n_chunk
            w_load(j).wait()
            weight_stack(wbuf[j % 2], stack)

            @pl.when(j + 2 < n_dx)
            def _():
                w_load(j + 2).start()

            @pl.when(j >= 2)
            def _():
                dx_store(j - 2).wait()

            xbuf[j % 2] = jnp.dot(
                cols_ref[...], stack[...], preferred_element_type=jnp.float32).astype(jnp.bfloat16)
            dx_store(j).start()

        return carry

    lax.fori_loop(0, n_chunk + WAIT_AG[0], step, 0)
    dx_store(n_dx - 2).wait()
    dx_store(n_dx - 1).wait()

    def finish(c, carry):
        dw_store(c).wait()
        return carry

    lax.fori_loop(0, n_chunk, finish, 0)
    cols_copy.wait()


def last_kernel(cols_ref, w_ref, dw_in, dx_in, dw_ref, dx_ref,
                wbuf, stack, obuf, dwbuf, dxbuf, w_sem, o_sem, dwi, dwo, dxi, dxo):
    n_chunk, n_done = dw_in.shape[0], dx_in.shape[0]
    n_left = n_chunk - n_done

    def cols(c):
        return pl.ds(pl.multiple_of(c * COLS, COLS), COLS)

    def w_load(j):
        return pltpu.make_async_copy(w_ref.at[:, cols(n_done + j)], wbuf.at[j], w_sem.at[j])

    def dw_load(c):
        return pltpu.make_async_copy(dw_in.at[c], dwbuf.at[c], dwi.at[c])

    def dw_store(c):
        return pltpu.make_async_copy(dwbuf.at[c], dw_ref.at[:, cols(c)], dwo.at[c])

    def dx_load(c):
        return pltpu.make_async_copy(dx_in.at[c], dxbuf.at[c], dxi.at[c])

    def dx_move(c):
        return pltpu.make_async_copy(dxbuf.at[c], dx_ref.at[:, cols(c)], dxo.at[c])

    def dx_store(j):
        return pltpu.make_async_copy(obuf.at[j % 2], dx_ref.at[:, cols(n_done + j)], o_sem.at[j % 2])

    def each(n, fn):
        lax.fori_loop(0, n, lambda k, carry: (fn(k), carry)[1], 0)

    each(n_left, lambda j: w_load(j).start())
    each(n_done, lambda c: dx_load(c).start())
    each(n_chunk, lambda c: dw_load(c).start())

    def move(load, store, c):
        load(c).wait()
        store(c).start()

    def step(j, carry):
        w_load(j).wait()
        weight_stack(wbuf[j], stack)

        @pl.when(j >= 2)
        def _():
            dx_store(j - 2).wait()

        obuf[j % 2] = jnp.dot(
            cols_ref[...], stack[...], preferred_element_type=jnp.float32).astype(jnp.bfloat16)
        dx_store(j).start()

        @pl.when(j == 0)
        def _():
            each(n_done, lambda c: move(dx_load, dx_move, c))

        @pl.when(j == 1)
        def _():
            each(n_chunk, lambda c: move(dw_load, dw_store, c))

        return carry

    lax.fori_loop(0, n_left, step, 0)
    dx_store(n_left - 2).wait()
    dx_store(n_left - 1).wait()
    each(n_done, lambda c: dx_move(c).wait())
    each(n_chunk, lambda c: dw_store(c).wait())


def solution(mesh):
    cp_size = mesh.shape["cp"]
    dp_size = mesh.shape["dp"]

    def local_step(tokens, choices, router_w, expert_bias):
        pieces_n, seq, dim = tokens.shape
        rows_all = pieces_n * dp_size
        seq_all = seq * cp_size
        experts = router_w.shape[0]
        choice_num = choices.shape[2]
        tok_n = pieces_n * seq
        n_chunk = dim // COLS
        n_dx = n_chunk - 5
        f32, bf16 = jnp.float32, jnp.bfloat16
        dma, any_shape = pltpu.SemaphoreType.DMA, jax.ShapeDtypeStruct
        flat = tokens.reshape(tok_n, dim)

        expert_ids = jnp.arange(experts, dtype=jnp.int32)
        counts = jnp.sum((choices[..., None] == expert_ids).astype(f32), axis=(1, 2))
        counts = jnp.concatenate([counts, jnp.zeros_like(counts)], axis=0)
        scale = ALPHA * experts / (rows_all * choice_num * seq_all * seq_all)
        got = [pltpu.VMEM((n_chunk, experts >> (k + 1), COLS), f32) for k in range(LEVELS - 1)]
        got.append(pltpu.VMEM((n_chunk, experts >> (LEVELS - 1), COLS // 2), f32))
        dw_sum, dx_done, grad_cols, small_sum = pl.pallas_call(
            functools.partial(main_kernel, n_dx, pieces_n, scale),
            out_shape=(any_shape((n_chunk, experts, COLS), f32), any_shape((n_dx, tok_n, COLS), bf16),
                       any_shape((tok_n, 6 * experts), bf16), any_shape((8, experts), f32)),
            in_specs=[VMEM, ANY, ANY], out_specs=(ANY, ANY, ANY, VMEM),
            scratch_shapes=[
                pltpu.VMEM((n_chunk, experts, COLS), f32), pltpu.VMEM((n_chunk, experts, COLS), f32), *got,
                pltpu.VMEM((2, tok_n, COLS), bf16), pltpu.VMEM((2, experts, COLS), f32),
                pltpu.VMEM((6 * experts, COLS), bf16), pltpu.VMEM((experts, tok_n), f32),
                pltpu.VMEM((3 * experts, tok_n), bf16), pltpu.VMEM((tok_n, 6 * experts), bf16),
                pltpu.VMEM((3, 8, experts), f32), pltpu.VMEM((2, 8, experts), f32),
                pltpu.VMEM((LEVELS, 8, experts), f32), pltpu.VMEM((LEVELS, 8, experts), f32),
                dma((LEVELS, n_chunk)), dma((LEVELS, n_chunk)), dma((LEVELS, n_chunk)),
                dma((LEVELS, n_chunk)), dma((LEVELS,)), dma((LEVELS,)), dma((2,)), dma((2,)),
                dma((2,)), dma((2,)), dma((2,)), dma((n_chunk,)), dma],
            compiler_params=pltpu.CompilerParams(
                collective_id=0, has_side_effects=True, vmem_limit_bytes=60 << 20),
        )(counts, flat, router_w)

        grad_router, grad_tokens = pl.pallas_call(
            last_kernel,
            out_shape=(any_shape((experts, dim), f32), any_shape((tok_n, dim), bf16)),
            in_specs=[VMEM, ANY, ANY, ANY], out_specs=(ANY, ANY),
            scratch_shapes=[
                pltpu.VMEM((n_chunk - n_dx, experts, COLS), f32), pltpu.VMEM((6 * experts, COLS), bf16),
                pltpu.VMEM((2, tok_n, COLS), bf16), pltpu.VMEM((n_chunk, experts, COLS), f32),
                pltpu.VMEM((n_dx, tok_n, COLS), bf16),
                dma((n_chunk - n_dx,)), dma((2,)), dma((n_chunk,)), dma((n_chunk,)),
                dma((n_dx,)), dma((n_dx,))],
            compiler_params=pltpu.CompilerParams(vmem_limit_bytes=44 << 20),
        )(grad_cols, router_w, dw_sum, dx_done)

        bal_loss = small_sum[1, 0]
        load_gap = rows_all * seq_all * choice_num - experts * small_sum[0].astype(jnp.int32)
        new_bias = expert_bias + GAMMA * jnp.sign(load_gap).astype(f32)
        return bal_loss, grad_router, grad_tokens.reshape(tokens.shape), new_bias

    tok_spec = P("dp", "cp", None)
    return jax.shard_map(local_step, mesh=mesh, in_specs=(tok_spec, tok_spec, P(), P()), out_specs=(P(), P(), tok_spec, P()), check_vma=False)
```

time: 321 us -> 186 us (0.58)
  Pallas kernels: 0 us -> 176 us
  matrix products: 142 us -> 0 us
  waiting for transfers between devices: 114 us -> 0 us
  blocking collectives: 35.2 us -> 0 us
  between operations: 14.1 us -> 0.66 us
  local copies, waits for them, and re-layouts: 10.7 us -> 5.86 us
    pallas_call x0 -> x2, Pallas kernels: none -> 176 us  [the longest x1 145 us: local_step(): pl.pallas_call(functools.partial(main_kernel, n_dx, pieces_n, scale), out...]
    dot_general x3 -> x0, matrix products: 142 us -> none  [the longest x1 77.1 us: local_step(): jnp.einsum('bsn,nd->bsd', grad_logits, router_w, precision=PRECISE, prefe...]
    psum x1 -> x0, waiting for transfers between devices: 114 us -> none  [local_step(): grad_router = lax.psum(grad_part, ('cp', 'dp'))]
    psum x3 -> x0, blocking collectives: 35.2 us -> none  [the longest x1 13.7 us: local_step(): seq_counts = lax.psum(piece_counts, 'cp')]
    unnamed x4 -> x5, local copies, waits for them, and re-layouts: 10.7 us -> 4.07 us
  transfers between devices with their start and end apart: 1 -> 0, of which waited for: 1 -> 0; matrix products, arithmetic and copies ran while one was open for 24% -> 0% of each run, Pallas kernels for 0% -> 0%
where the time goes in v1:
time: 186 us
  Pallas kernels  176 us (95%)
  local copies, waits for them, and re-layouts  5.86 us (3%)
  other arithmetic  3.82 us (2%)
    pallas_call x1, Pallas kernels, local_step(): pl.pallas_call(functools.partial(main_kernel, n_dx, pieces_n, scale), out...  145 us
    pallas_call x1, Pallas kernels, local_step(): pl.pallas_call(last_kernel, out_shape=(any_shape((experts, dim), f32), an...  30.7 us
    unnamed x5, local copies, waits for them, and re-layouts  4.07 us

profile of v1, /device:TPU:0, one launch (start us, length us, event | category | flops | bytes accessed | tf_op | source)
XLA Modules:
  0.0 186.0 jit_solution(7664872189305890508)
XLA Ops:
  0.6 1.1 copy.9
  1.7 2.5 %convert_reduce_fusion = f32[4,384]{1,0:T(4,128)S(1)} fusion(s32[4,384,8]{2,1,0:T(8,128)S(1)} %copy.9), kind=kLoop, calls=%fused_computation | loop fusion | flops 14154240 | bytes 55296 | tf_op jit(solution)/shard_map/reduce_sum | solution.py:351
  4.2 0.6 concatenate.3.cnt_ref
  4.8 0.0 copy-start.1
  4.8 144.9 %shard_map.75 = (f32[14,384,512]{2,1,0:T(8,128)}, bf16[9,1536,512]{2,1,0:T(8,128)(2,1)}, bf16[1536,2304]{1,0:T(8,128)(2,1)}, f32[8,384]{1,0:T(8,128)}) custom-call(f32[8,384]{1,0:T(8,128)} %concatenate.3.cnt_ref, bf16[1536,7168]{1,0:T(8,128)(2,1)} %bitcast.3, f32[384,7168]{1,0:T(8,128)} %w_ref.3), custom_call_target="tpu_custom_call" | custom-call | tf_op jit(solution)/shard_map/pallas_call | solution.py:356
  149.7 1.2 slice.6
  150.9 0.7 multiply_reduce_fusion
  151.6 0.0 copy-done.1
  151.7 0.6 add.5
  152.2 0.0 copy-start
  152.2 3.0 %copy-done = bf16[1536,2304]{1,0:T(8,128)(2,1)S(1)} copy-done((bf16[1536,2304]{1,0:T(8,128)(2,1)S(1)}, bf16[1536,2304]{1,0:T(8,128)(2,1)}, u32[]{:S(2)}) %copy-start) | copy-done | bytes 7077912
  155.2 30.7 %shard_map.76 = (f32[384,7168]{1,0:T(8,128)}, bf16[1536,7168]{1,0:T(8,128)(2,1)}) custom-call(bf16[1536,2304]{1,0:T(8,128)(2,1)S(1)} %copy-done, f32[384,7168]{1,0:T(8,128)} %w_ref.3, f32[14,384,512]{2,1,0:T(8,128)} %get-tuple-element.12.dw_in, bf16[9,1536,512]{2,1,0:T(8,128)(2,1)} %get-tuple-element.13.dx_in), custom_call_target="tpu_custom_call" | custom-call | tf_op jit(solution)/shard_map/pallas_call | solution.py:375
Async XLA Ops:
  4.8 146.8 %copy-start.1 = (f32[384]{0:T(512)S(1)}, f32[384]{0:T(512)}, u32[]{:S(2)}) copy-start(f32[384]{0:T(512)} %param.7) | copy-start | bytes 4612
  152.2 3.0 %copy-start = (bf16[1536,2304]{1,0:T(8,128)(2,1)S(1)}, bf16[1536,2304]{1,0:T(8,128)(2,1)}, u32[]{:S(2)}) copy-start(bf16[1536,2304]{1,0:T(8,128)(2,1)} %get-tuple-element.11.cols_ref) | copy-start | bytes 21233668

commit v2 on v1

--- a/solution.py
+++ b/solution.py
@@ -33,11 +33,11 @@
         stack[pl.ds(k * experts, experts), :] = parts[which]
 
 
-def main_kernel(n_dx, seqs, scale, cnt_ref, x_ref, w_ref, dw_ref, dx_ref, cols_out, small_out,
-                acc, full, got0, got1, got2, got3, got4, xbuf, wbuf, stack, scores, rows_ref, cols_ref,
+def main_kernel(n_dx, seqs, scale, cnt_ref, x_ref, w_ref, dw_ref, dx_ref, cols_ref, small_out,
+                acc, full, got0, got1, got2, got3, got4, xbuf, wbuf, stack, scores, rows_ref,
                 cnt_cur, cnt_got, small_cur, small_got,
                 rs_send, rs_recv, ag_send, ag_recv, sm_send, sm_recv, cnt_send, cnt_recv,
-                x_sem, w_sem, o_sem, d_sem, c_sem):
+                x_sem, w_sem, o_sem, d_sem):
     n_chunk, experts = acc.shape[0], acc.shape[1]
     tok_n = xbuf.shape[1]
     seq = tok_n // seqs
@@ -168,8 +168,6 @@
         return carry
 
     lax.fori_loop(0, seqs, grad_step, 0)
-    cols_copy = pltpu.make_async_copy(cols_ref, cols_out, c_sem)
-    cols_copy.start()
 
     def step(i, carry):
         def at(offset):
@@ -261,7 +259,6 @@
         return carry
 
     lax.fori_loop(0, n_chunk, finish, 0)
-    cols_copy.wait()
 
 
 def last_kernel(cols_ref, w_ref, dw_in, dx_in, dw_ref, dx_ref,
@@ -342,7 +339,7 @@
         choice_num = choices.shape[2]
         tok_n = pieces_n * seq
         n_chunk = dim // COLS
-        n_dx = n_chunk - 5
+        n_dx = n_chunk - 4
         f32, bf16 = jnp.float32, jnp.bfloat16
         dma, any_shape = pltpu.SemaphoreType.DMA, jax.ShapeDtypeStruct
         flat = tokens.reshape(tok_n, dim)
@@ -357,19 +354,19 @@
             functools.partial(main_kernel, n_dx, pieces_n, scale),
             out_shape=(any_shape((n_chunk, experts, COLS), f32), any_shape((n_dx, tok_n, COLS), bf16),
                        any_shape((tok_n, 6 * experts), bf16), any_shape((8, experts), f32)),
-            in_specs=[VMEM, ANY, ANY], out_specs=(ANY, ANY, ANY, VMEM),
+            in_specs=[VMEM, ANY, ANY], out_specs=(ANY, ANY, VMEM, VMEM),
             scratch_shapes=[
                 pltpu.VMEM((n_chunk, experts, COLS), f32), pltpu.VMEM((n_chunk, experts, COLS), f32), *got,
                 pltpu.VMEM((2, tok_n, COLS), bf16), pltpu.VMEM((2, experts, COLS), f32),
                 pltpu.VMEM((6 * experts, COLS), bf16), pltpu.VMEM((experts, tok_n), f32),
-                pltpu.VMEM((3 * experts, tok_n), bf16), pltpu.VMEM((tok_n, 6 * experts), bf16),
+                pltpu.VMEM((3 * experts, tok_n), bf16),
                 pltpu.VMEM((3, 8, experts), f32), pltpu.VMEM((2, 8, experts), f32),
                 pltpu.VMEM((LEVELS, 8, experts), f32), pltpu.VMEM((LEVELS, 8, experts), f32),
                 dma((LEVELS, n_chunk)), dma((LEVELS, n_chunk)), dma((LEVELS, n_chunk)),
                 dma((LEVELS, n_chunk)), dma((LEVELS,)), dma((LEVELS,)), dma((2,)), dma((2,)),
-                dma((2,)), dma((2,)), dma((2,)), dma((n_chunk,)), dma],
+                dma((2,)), dma((2,)), dma((2,)), dma((n_chunk,))],
             compiler_params=pltpu.CompilerParams(
-                collective_id=0, has_side_effects=True, vmem_limit_bytes=60 << 20),
+                collective_id=0, has_side_effects=True, vmem_limit_bytes=47 << 20),
         )(counts, flat, router_w)
 
         grad_router, grad_tokens = pl.pallas_call(
@@ -382,7 +379,7 @@
                 pltpu.VMEM((n_dx, tok_n, COLS), bf16),
                 dma((n_chunk - n_dx,)), dma((2,)), dma((n_chunk,)), dma((n_chunk,)),
                 dma((n_dx,)), dma((n_dx,))],
-            compiler_params=pltpu.CompilerParams(vmem_limit_bytes=44 << 20),
+            compiler_params=pltpu.CompilerParams(vmem_limit_bytes=38 << 20),
         )(grad_cols, router_w, dw_sum, dx_done)
 
         bal_loss = small_sum[1, 0]

time: 186 us -> 178 us (0.957)
  local copies, waits for them, and re-layouts: 5.86 us -> 1.58 us
  Pallas kernels: 176 us -> 172 us
    pallas_call x1, Pallas kernels: 30.7 us -> 27.4 us  [local_step(): pl.pallas_call(last_kernel, out_shape=(any_shape((experts, dim), f32), an...]
    unnamed x5 -> x3, local copies, waits for them, and re-layouts: 4.07 us -> 1.07 us
where the time goes in v2:
time: 178 us; the launch traced here: 177 us
  Pallas kernels  172 us (97%)
  other arithmetic  3.12 us (2%)
    pallas_call x1, Pallas kernels, local_step(): pl.pallas_call(functools.partial(main_kernel, n_dx, pieces_n, scale), out...  145 us
    pallas_call x1, Pallas kernels, local_step(): pl.pallas_call(last_kernel, out_shape=(any_shape((experts, dim), f32), an...  27.4 us

profile of v2, /device:TPU:0, one launch (start us, length us, event | category | flops | bytes accessed | tf_op | source)
XLA Modules:
  0.0 177.4 jit_solution(5468140411172458607)
XLA Ops:
  0.6 1.1 copy.9
  1.7 2.5 %convert_reduce_fusion = f32[4,384]{1,0:T(4,128)S(1)} fusion(s32[4,384,8]{2,1,0:T(8,128)S(1)} %copy.9), kind=kLoop, calls=%fused_computation | loop fusion | flops 14154240 | bytes 55296 | tf_op jit(solution)/shard_map/reduce_sum | solution.py:348
  4.2 144.6 %shard_map.75 = (f32[14,384,512]{2,1,0:T(8,128)}, bf16[10,1536,512]{2,1,0:T(8,128)(2,1)}, bf16[1536,2304]{1,0:T(8,128)(2,1)S(1)}, f32[8,384]{1,0:T(8,128)S(1)}) custom-call(f32[8,384]{1,0:T(8,128)S(1)} %concatenate.3.cnt_ref, bf16[1536,7168]{1,0:T(8,128)(2,1)} %bitcast.3, f32[384,7168]{1,0:T(8,128)} %w_ref.3), custom_call_target="tpu_custom_call" | custom-call | tf_op jit(solution)/shard_map/pallas_call | solution.py:353
  148.9 0.0 copy-start
  148.9 27.4 %shard_map.76 = (f32[384,7168]{1,0:T(8,128)}, bf16[1536,7168]{1,0:T(8,128)(2,1)}) custom-call(bf16[1536,2304]{1,0:T(8,128)(2,1)S(1)} %get-tuple-element.11.cols_ref, f32[384,7168]{1,0:T(8,128)} %w_ref.3, f32[14,384,512]{2,1,0:T(8,128)} %get-tuple-element.12.dw_in, bf16[10,1536,512]{2,1,0:T(8,128)(2,1)} %get-tuple-element.13.dx_in), custom_call_target="tpu_custom_call" | custom-call | tf_op jit(solution)/shard_map/pallas_call | solution.py:372
  176.3 0.0 copy-done
  176.3 0.6 add.5
  176.9 0.5 slice.6
  (2 shorter events, 0.0 us)
Async XLA Ops:
  148.9 27.5 %copy-start = (f32[384]{0:T(512)S(1)}, f32[384]{0:T(512)}, u32[]{:S(2)}) copy-start(f32[384]{0:T(512)} %param.7) | copy-start | bytes 4612
